TPU v7x, 32 devices: a whole 2x2x4 slice. The times are simulated.
32 devices in a mesh: req: 8 (over z, core), blk: 4 (over y, x).
Axes of the slice: x: 2, y: 2, z: 4, core: 2. Of those that a mesh axis runs over, the one named last changes fastest.
Arguments:
- draft_node_queries: bfloat16 [256, 4096], P(('req', 'blk')), parts along dimension 0, may hold values from -6 to 6, as said below
- draft_node_keys: bfloat16 [256, 512], P(('req', 'blk')), parts along dimension 0, may hold values from -6 to 6
- draft_node_values: bfloat16 [256, 512], P(('req', 'blk')), parts along dimension 0, may hold values from -6 to 6
- paged_key_cache: bfloat16 [16384, 512], P(('req', 'blk')), parts along dimension 0, may hold values from -6 to 6
- paged_value_cache: bfloat16 [16384, 512], P(('req', 'blk')), parts along dimension 0, may hold values from -6 to 6
- context_length: int32 [8], P('req'), parts along dimension 0, may hold values from 1024 to 2048
- parents: int32 [256], P('req'), parts along dimension 0, may hold values from 0 to 31, as said below
- accepted_path: int32 [64], P('req'), parts along dimension 0, may hold values from 0 to 31, as said below
- out_weight: bfloat16 [2880, 4096], P('blk'), may hold values from -0.09375 to 0.09375
Outputs:
- tree_attention: bfloat16 [256, 4096], P(('req', 'blk')), parts along dimension 0
- path_output: bfloat16 [64, 2880], P('req', 'blk'), parts along dimension 0
There are 8 independent parts, one for each index of `req`. A program takes and returns all parts, laid end to end along the dimension named above; an argument that names none is the same for every part. Nothing has to cross between parts.
Inputs may be any that keep to these rules, and one draw needn't show every extreme that they name: `draft_node_queries`: query entries lie within the range. parents[0] = 0 marks the root; for i >= 1, parents[i] is one of the nodes i - 4 to i - 1 (and at least 0). `accepted_path`: distinct nodes; each entry after the first is a child of the one before it.
All inputs are finite; a program needn't handle non-finite values.
Results may differ from a plain program's by a relative error of at most 0.0095.
Values may be sent and summed in bfloat16 or wider, within the bound.
A program may use at most 64 MiB of HBM per device.

v0:
```python
import jax
import jax.numpy as jnp
from jax import lax
from jax.sharding import PartitionSpec as P

QUERY_HEADS = 64
KEY_VALUE_HEADS = 8
HEAD_WIDTH = 64


score_after_mask = -1e30


def ancestors(parents):
    draft_node_count = parents.shape[0]
    indices = jnp.arange(draft_node_count, dtype=jnp.int32)
    linked = (parents[:, None] == indices[None, :]) & (indices[:, None] > 0)
    ancestry = jnp.minimum(
        jnp.eye(draft_node_count, dtype=jnp.float32) + linked.astype(jnp.float32), 1.0
    )
    for squaring in range(7):
        ancestry = jnp.minimum(jnp.dot(ancestry, ancestry, precision=lax.Precision.HIGHEST), 1.0)
    return ancestry > 0.5


def fresh_state(cache_row_count):
    query_group_width = QUERY_HEADS // KEY_VALUE_HEADS
    return (
        jnp.full(
            (cache_row_count, KEY_VALUE_HEADS, query_group_width), score_after_mask, jnp.float32
        ),
        jnp.zeros((cache_row_count, KEY_VALUE_HEADS, query_group_width), jnp.float32),
        jnp.zeros((cache_row_count, KEY_VALUE_HEADS, query_group_width, HEAD_WIDTH), jnp.float32),
    )


def combine(first_part, second_part):
    maxima = jnp.maximum(first_part[0], second_part[0])
    first_scale = jnp.exp(first_part[0] - maxima)
    second_scale = jnp.exp(second_part[0] - maxima)
    totals = first_part[1] * first_scale + second_part[1] * second_scale
    weighted = first_part[2] * first_scale[..., None] + second_part[2] * second_scale[..., None]
    return (maxima, totals, weighted)


def fold_block(state, grouped_queries, flat_key_rows, flat_value_rows, usable):
    maxima, totals, weighted = state
    cache_row_count = flat_key_rows.shape[0]
    gathered_key_block = flat_key_rows.reshape(cache_row_count, KEY_VALUE_HEADS, HEAD_WIDTH)
    gathered_value_block = flat_value_rows.reshape(cache_row_count, KEY_VALUE_HEADS, HEAD_WIDTH)
    scores = jnp.einsum(
        "mrjz,xrz->mrjx", grouped_queries, gathered_key_block, preferred_element_type=jnp.float32
    ) * HEAD_WIDTH ** (-0.5)
    scores = jnp.where(usable, scores, score_after_mask)
    new_maxima = jnp.maximum(maxima, jnp.max(scores, axis=-1))
    weights = jnp.where(usable, jnp.exp(scores - new_maxima[..., None]), 0.0)
    rescale = jnp.exp(maxima - new_maxima)
    totals = totals * rescale + jnp.sum(weights, axis=-1)
    weighted = weighted * rescale[..., None] + jnp.einsum(
        "zvle,evt->zvlt",
        weights.astype(jnp.bfloat16),
        gathered_value_block,
        preferred_element_type=jnp.float32,
    )
    return (new_maxima, totals, weighted)


def cache_partial(grouped_queries, paged_key_cache, paged_value_cache, offset, length, state):
    rows_per_block = min(512, paged_key_cache.shape[0])
    block_table = paged_key_cache.shape[0] // rows_per_block
    gathered_key_blocks = paged_key_cache.reshape(
        block_table, rows_per_block, paged_key_cache.shape[1]
    )
    gathered_value_blocks = paged_value_cache.reshape(
        block_table, rows_per_block, paged_value_cache.shape[1]
    )
    starts = offset + rows_per_block * jnp.arange(block_table, dtype=jnp.int32)

    def step_fn(carried, pieces):
        usable = pieces[2] + jnp.arange(rows_per_block, dtype=jnp.int32) < length
        return (fold_block(carried, grouped_queries, pieces[0], pieces[1], usable), None)

    result, unused = lax.scan(step_fn, state, (gathered_key_blocks, gathered_value_blocks, starts))
    return result


def tree_partial(grouped_queries, keys_all, values_all, ancestry_rows):
    return fold_block(
        fresh_state(grouped_queries.shape[0]),
        grouped_queries,
        keys_all,
        values_all,
        ancestry_rows[:, None, None, :],
    )


def normalize(partial_value):
    cache_row_count = partial_value[2].shape[0]
    return (
        (partial_value[2] / partial_value[1][..., None])
        .astype(jnp.bfloat16)
        .reshape(cache_row_count, QUERY_HEADS * HEAD_WIDTH)
    )


def local(
    draft_node_queries,
    draft_node_keys,
    draft_node_values,
    paged_key_cache,
    paged_value_cache,
    context_length,
    parents,
    accepted_path,
    out_weight,
):
    own_rows = draft_node_queries.shape[0]
    draft_node_count = parents.shape[0]
    query_group_width = QUERY_HEADS // KEY_VALUE_HEADS
    position = lax.axis_index("blk")
    offset = position * paged_key_cache.shape[0]
    length = context_length[0]
    ancestry = ancestors(parents)
    own_ancestry = lax.dynamic_slice_in_dim(ancestry, position * own_rows, own_rows, 0)
    own_queries = draft_node_queries.reshape(
        own_rows, KEY_VALUE_HEADS, query_group_width, HEAD_WIDTH
    )
    every_query_row, keys_all, values_all = (
        lax.all_gather(draft_node_queries, "blk", axis=0, tiled=True),
        lax.all_gather(draft_node_keys, "blk", axis=0, tiled=True),
        lax.all_gather(draft_node_values, "blk", axis=0, tiled=True),
    )
    grouped_queries = every_query_row.reshape(
        draft_node_count, KEY_VALUE_HEADS, query_group_width, HEAD_WIDTH
    )
    partial_value = cache_partial(
        grouped_queries,
        paged_key_cache,
        paged_value_cache,
        offset,
        length,
        fresh_state(draft_node_count),
    )
    arrived = (
        lax.all_to_all(partial_value[0][None], "blk", split_axis=1, concat_axis=0, tiled=True),
        lax.all_to_all(partial_value[1][None], "blk", split_axis=1, concat_axis=0, tiled=True),
        lax.all_to_all(partial_value[2][None], "blk", split_axis=1, concat_axis=0, tiled=True),
    )
    maxima = jnp.max(arrived[0], axis=0)
    scales = jnp.exp(arrived[0] - maxima[None])
    totals = jnp.sum(arrived[1] * scales, axis=0)
    weighted = jnp.sum(arrived[2] * scales[..., None], axis=0)
    partial_value = combine(
        (maxima, totals, weighted), tree_partial(own_queries, keys_all, values_all, own_ancestry)
    )
    attention_own = normalize(partial_value)
    attention_all = lax.all_gather(attention_own, "blk", axis=0, tiled=True)
    picker = (
        accepted_path[:, None] == jnp.arange(draft_node_count, dtype=jnp.int32)[None, :]
    ).astype(jnp.bfloat16)
    path_rows = jnp.dot(picker, attention_all, preferred_element_type=jnp.float32).astype(
        jnp.bfloat16
    )
    path_output = lax.dot_general(
        path_rows, out_weight, (((1,), (1,)), ((), ())), preferred_element_type=jnp.float32
    ).astype(jnp.bfloat16)
    return (attention_own, path_output)


def solution(mesh):
    in_specs = (
        P(("req", "blk"), None),
        P(("req", "blk"), None),
        P(("req", "blk"), None),
        P(("req", "blk"), None),
        P(("req", "blk"), None),
        P("req"),
        P("req"),
        P("req"),
        P("blk", None),
    )
    out_specs = (P(("req", "blk"), None), P("req", "blk"))
    return jax.shard_map(local, mesh=mesh, in_specs=in_specs, out_specs=out_specs, check_vma=False)
```

profile of v0, /device:TPU:0, one launch (start us, length us, event | category | flops | bytes accessed | tf_op | source)
XLA Modules:
  0.0 78.9 jit_solution(13678298688536361862)
XLA Ops:
  1.3 10.8 %all_gather.12 = bf16[32,4096]{1,0:T(8,128)(2,1)S(1)} all-gather(bf16[8,4096]{1,0:T(8,128)(2,1)} %param.9), channel_id=1, replica_groups=mesh['req'=8,'blk'=4] {'blk'}, dimensions={0}, use_global_device_ids=true | all-gather | bytes 327680 | tf_op jit(solution)/shard_map/all_gather | solution.py:129
  12.0 0.5 reshape.137
  12.6 1.3 %copy.73 = bf16[512,512]{0,1:T(8,128)(2,1)S(1)} copy(bf16[512,512]{1,0:T(8,128)(2,1)} %param.12) | data formatting | bytes 1048576 | tf_op args[3]
  13.9 0.9 %bitcast_reduce_fusion = (f32[32,8,8]{0,2,1:T(8,128)S(1)}, f32[8,512,32,8]{1,2,3,0:T(8,128)S(1)}) fusion(pred[512]{0:T(512)(128)(4,1)S(1)} %add_compare_fusion, bf16[512,8,64,1]{0,2,3,1:T(8,128)(2,1)S(1)} %bitcast.85, bf16[32,8,8,64]{3,2,1,0:T(8,128)(2,1)S(1)} %reshape.137), kind=kOutput, calls=%fused_computation.2 | convolution fusion | flops 137361408 | bytes 4989440 | tf_op jit(solution)/shard_map/while/body/eval_jaxpr/mrjz,xrz->mrjx/dot_general | solution.py:51
  14.8 0.0 copy-start.6
  14.8 0.0 copy-start.3
  14.8 0.0 copy-start
  14.8 1.4 %fusion.2 = (f32[32,8,8]{0,2,1:T(8,128)S(1)}, bf16[32,8,8,512]{3,0,2,1:T(8,128)(2,1)S(1)}) fusion(f32[8,512,32,8]{1,2,3,0:T(8,128)S(1)} %get-tuple-element.41, f32[32,8,8]{0,2,1:T(8,128)S(1)} %get-tuple-element.39, pred[512]{0:T(512)(128)(4,1)S(1)} %add_compare_fusion), kind=kLoop, calls=%fused_computation.6 | loop fusion | flops 6289408 | bytes 6308352 | tf_op jit(solution)/shard_map/while/body/eval_jaxpr/reduce_sum | solution.py:58
  16.2 0.1 copy.91
  16.4 0.7 reshape.151
  17.1 3.2 %all-to-all-start.2 = ((f32[4,1,512]{2,1,0:T(1,128)}), f32[4,1,512]{2,1,0:T(1,128)S(1)}, u32[]{:S(2)}, u32[]{:S(2)}) async-start(f32[4,1,512]{2,1,0:T(1,128)} %reshape.151), calls=%async_computation.2 | async-start | bytes 16384 | tf_op jit(solution)/shard_map/all_to_all | solution.py:146
  20.3 0.0 copy-done.1
  20.4 0.2 reshape.140
  20.5 0.0 copy-done.6
  20.5 0.2 convolution_minimum_fusion.5
  20.8 0.1 convolution_minimum_fusion.4
  20.9 0.1 convolution_minimum_fusion.3
  21.1 0.1 convolution_minimum_fusion.2
  21.2 0.1 convolution_minimum_fusion.1
  21.4 0.1 convolution_minimum_fusion
  21.5 0.1 fusion.55
  21.7 0.0 copy-done.3
  21.7 8.7 %all_gather.13 = bf16[32,512]{1,0:T(8,128)(2,1)S(1)} all-gather(bf16[8,512]{1,0:T(8,128)(2,1)S(1)} %copy-done.3), channel_id=1, replica_groups=mesh['req'=8,'blk'=4] {'blk'}, dimensions={0}, use_global_device_ids=true | all-gather | bytes 40960 | tf_op jit(solution)/shard_map/all_gather | solution.py:130
  30.3 0.1 reshape.139
  30.5 0.3 fusion.54
  30.7 0.1 copy.84
  30.8 0.1 copy.88
  30.9 0.8 copy.75
  31.7 0.0 copy-done
  31.7 1.0 %copy.76 = bf16[512,512]{0,1:T(8,128)(2,1)} copy(bf16[512,512]{1,0:T(8,128)(2,1)S(1)} %copy-done) | data formatting | bytes 1048576 | tf_op args[4]
  32.7 2.4 %fusion.12 = f32[1,32,8,8,64]{4,3,1,2,0:T(8,128)S(1)} fusion(bf16[512,8,64,1]{0,2,3,1:T(8,128)(2,1)} %bitcast.91, bf16[32,8,8,512]{3,0,2,1:T(8,128)(2,1)S(1)} %get-tuple-element.26, f32[32,8,8]{2,0,1:T(8,128)} %copy.75), kind=kOutput, calls=%fused_computation.12 | convolution fusion | flops 134348800 | bytes 3153920 | tf_op jit(solution)/shard_map/while/body/eval_jaxpr/zvle,evt->zvlt/dot_general | solution.py:59
  35.1 0.3 fusion.26
  35.4 0.1 copy.79
  35.5 0.7 reshape.149
  36.2 0.1 copy.93
  36.3 0.1 copy.132
  36.4 1.4 %reshape.147 = f32[4,1,32768]{2,1,0:T(1,128)} reshape(f32[32,1,8,8,64]{4,3,2,1,0:T(8,128)S(1)} %bitcast.84) | data formatting | bytes 1048576
  37.9 0.0 all-to-all-done.2
  37.9 3.2 %all-to-all-start.1 = ((f32[4,1,512]{2,1,0:T(1,128)}), f32[4,1,512]{2,1,0:T(1,128)S(1)}, u32[]{:S(2)}, u32[]{:S(2)}) async-start(f32[4,1,512]{2,1,0:T(1,128)} %reshape.149), calls=%async_computation.1 | async-start | bytes 16384 | tf_op jit(solution)/shard_map/all_to_all | solution.py:145
  41.1 0.0 copy-done.4
  41.1 8.6 %all_gather.14 = bf16[32,512]{1,0:T(8,128)(2,1)S(1)} all-gather(bf16[8,512]{1,0:T(8,128)(2,1)S(1)} %copy-done.4), channel_id=1, replica_groups=mesh['req'=8,'blk'=4] {'blk'}, dimensions={0}, use_global_device_ids=true | all-gather | bytes 40960 | tf_op jit(solution)/shard_map/all_gather | solution.py:131
  49.8 0.1 reshape.141
  49.9 0.5 broadcast.122
  50.4 0.7 reduce.1
  51.1 0.1 reshape.152
  51.2 0.0 all-to-all-done.1
  51.2 3.5 %all-to-all-start = ((f32[4,1,32768]{2,1,0:T(1,128)}), f32[4,1,32768]{2,1,0:T(1,128)S(1)}, u32[]{:S(2)}, u32[]{:S(2)}) async-start(f32[4,1,32768]{2,1,0:T(1,128)} %reshape.147), calls=%async_computation | async-start | bytes 1048576 | tf_op jit(solution)/shard_map/all_to_all | solution.py:147
  54.7 0.7 reduce.2
  55.4 0.1 reshape.150
  55.5 0.1 copy.104
  55.6 0.1 copy.105
  55.7 0.1 copy.85
  55.8 0.1 copy.87
  55.9 0.1 copy.90
  56.0 0.1 copy.94
  56.0 5.2 %all-to-all-done = f32[4,1,32768]{2,1,0:T(1,128)S(1)} async-done(((f32[4,1,32768]{2,1,0:T(1,128)}), f32[4,1,32768]{2,1,0:T(1,128)S(1)}, u32[]{:S(2)}, u32[]{:S(2)}) %all-to-all-start) | async-done | bytes 524320 | tf_op jit(solution)/shard_map/all_to_all | solution.py:147
  61.2 2.1 %reduce = f32[4,32768]{1,0:T(4,128)S(1)} reduce(f32[4,1,32768]{2,1,0:T(1,128)S(1)} %all-to-all-done, f32[]{:T(128)} %broadcast.122), dimensions={1}, to_apply=%all_to_all.12.reduce_sub_computation | reduce | bytes 1048580 | tf_op jit(solution)/shard_map/all_to_all | solution.py:147
  63.4 0.5 reshape.148
  63.9 0.3 multiply_reduce_fusion
  64.3 0.4 fusion.21
  64.7 0.2 reshape.142
  64.9 0.0 copy-start.2
  64.9 9.0 %all_gather.15 = bf16[32,4096]{1,0:T(8,128)(2,1)S(1)} all-gather(bf16[8,4096]{1,0:T(8,128)(2,1)S(1)} %reshape.142), channel_id=1, replica_groups=mesh['req'=8,'blk'=4] {'blk'}, dimensions={0}, use_global_device_ids=true | all-gather | bytes 327680 | tf_op jit(solution)/shard_map/all_gather | solution.py:157
  73.9 5.0 %fusion.23 = bf16[8,720]{1,0:T(8,128)(2,1)} fusion(bf16[720,4096]{1,0:T(8,128)(2,1)} %param.17, bf16[32,4096]{1,0:T(8,128)(2,1)S(1)} %all_gather.15, s32[8]{0:T(128)S(1)} %copy-done.5), kind=kOutput, calls=%fused_computation.23 | convolution fusion | flops 49321856 | bytes 6171936 | tf_op jit(solution)/shard_map/dot_general | solution.py:164
  (15 shorter events, 0.2 us)
Async XLA Ops:
  14.8 5.6 %copy-start.1 = (bf16[8,4096]{1,0:T(8,128)(2,1)S(1)}, bf16[8,4096]{1,0:T(8,128)(2,1)}, u32[]{:S(2)}) copy-start(bf16[8,4096]{1,0:T(8,128)(2,1)} %param.9) | copy-start | bytes 196612
  14.8 5.8 %copy-start.6 = (s32[32]{0:T(128)S(1)}, s32[32]{0:T(128)}, u32[]{:S(2)}) copy-start(s32[32]{0:T(128)} %param.15) | copy-start | bytes 388
  14.8 6.9 %copy-start.3 = (bf16[8,512]{1,0:T(8,128)(2,1)S(1)}, bf16[8,512]{1,0:T(8,128)(2,1)}, u32[]{:S(2)}) copy-start(bf16[8,512]{1,0:T(8,128)(2,1)} %param.10) | copy-start | bytes 24580
  14.8 16.9 %copy-start = (bf16[512,512]{1,0:T(8,128)(2,1)S(1)}, bf16[512,512]{1,0:T(8,128)(2,1)}, u32[]{:S(2)}) copy-start(bf16[512,512]{1,0:T(8,128)(2,1)} %param.13) | copy-start | bytes 1572868
  17.1 20.8 %all-to-all-start.2 = ((f32[4,1,512]{2,1,0:T(1,128)}), f32[4,1,512]{2,1,0:T(1,128)S(1)}, u32[]{:S(2)}, u32[]{:S(2)}) async-start(f32[4,1,512]{2,1,0:T(1,128)} %reshape.151), calls=%async_computation.2 | async-start | bytes 16384 | tf_op jit(solution)/shard_map/all_to_all | solution.py:146
  32.7 8.5 %copy-start.4 = (bf16[8,512]{1,0:T(8,128)(2,1)S(1)}, bf16[8,512]{1,0:T(8,128)(2,1)}, u32[]{:S(2)}) copy-start(bf16[8,512]{1,0:T(8,128)(2,1)} %param.11) | copy-start | bytes 24580
  37.9 13.3 %all-to-all-start.1 = ((f32[4,1,512]{2,1,0:T(1,128)}), f32[4,1,512]{2,1,0:T(1,128)S(1)}, u32[]{:S(2)}, u32[]{:S(2)}) async-start(f32[4,1,512]{2,1,0:T(1,128)} %reshape.149), calls=%async_computation.1 | async-start | bytes 16384 | tf_op jit(solution)/shard_map/all_to_all | solution.py:145
  51.2 10.0 %all-to-all-start = ((f32[4,1,32768]{2,1,0:T(1,128)}), f32[4,1,32768]{2,1,0:T(1,128)S(1)}, u32[]{:S(2)}, u32[]{:S(2)}) async-start(f32[4,1,32768]{2,1,0:T(1,128)} %reshape.147), calls=%async_computation | async-start | bytes 1048576 | tf_op jit(solution)/shard_map/all_to_all | solution.py:147
  55.6 18.3 %copy-start.5 = (s32[8]{0:T(128)S(1)}, s32[8]{0:T(128)}, u32[]{:S(2)}) copy-start(s32[8]{0:T(128)} %param.16) | copy-start | bytes 100
  64.9 14.0 %copy-start.2 = (bf16[8,4096]{1,0:T(8,128)(2,1)}, bf16[8,4096]{1,0:T(8,128)(2,1)S(1)}, u32[]{:S(2)}) copy-start(bf16[8,4096]{1,0:T(8,128)(2,1)S(1)} %reshape.142) | copy-start | bytes 196612
where the time goes:
time: 79.5 us; the launch traced here: 78.9 us
  blocking collectives  37 us (47%)
  matrix products  10.1 us (13%)
  starting transfers between devices  9.98 us (13%)
  local copies, waits for them, and re-layouts  9.31 us (12%)
  other arithmetic  5.63 us (7%)
  waiting for transfers between devices  5.21 us (7%)
  between operations  1.63 us (2%)
    all_gather x1, blocking collectives, local(): lax.all_gather(draft_node_queries, 'blk', axis=0, tiled=True)  10.8 us
    all_gather x1, blocking collectives, local(): attention_all = lax.all_gather(attention_own, 'blk', axis=0, tiled=True)  8.98 us
    all_gather x1, blocking collectives, local(): lax.all_gather(draft_node_keys, 'blk', axis=0, tiled=True)  8.65 us
    all_gather x1, blocking collectives, local(): lax.all_gather(draft_node_values, 'blk', axis=0, tiled=True)  8.64 us
    unnamed x24, local copies, waits for them, and re-layouts  6.08 us
    all_to_all x1, waiting for transfers between devices, local(): lax.all_to_all(partial_value[2][None], 'blk', split_axis=1, concat_axis=0...  5.21 us
    dot_general x1, matrix products, local(): lax.dot_general(path_rows, out_weight, (((1,), (1,)), ((), ())), preferre...  5.04 us
    all_to_all x1, starting transfers between devices, local(): lax.all_to_all(partial_value[2][None], 'blk', split_axis=1, concat_axis=0...  3.48 us
  transfers between devices with their start and end apart: 3, of which 1 were waited for; matrix products, arithmetic and copies ran while one was open for 14% of the time, Pallas kernels for 0%

commit v1 on v0

v1 whole, which is shorter than its diff:
```python
import functools
import math

import jax
import jax.numpy as jnp
from jax import lax
from jax.experimental import pallas as pl
from jax.experimental.pallas import tpu as pltpu
from jax.sharding import PartitionSpec as P

QUERY_HEADS = 64
KEY_VALUE_HEADS = 8
HEAD_WIDTH = 64
GROUP = QUERY_HEADS // KEY_VALUE_HEADS
LANES = 128
CHUNKS = KEY_VALUE_HEADS * HEAD_WIDTH // LANES
CHUNK = 2 * GROUP * HEAD_WIDTH
PAIRS = CHUNK // LANES
EXCLUDED = -1e30
FLOOR = -1e20
SCALE = HEAD_WIDTH ** (-0.5)
NT = (((1,), (1,)), ((), ()))
MESH = pl.DeviceIdType.MESH


def kernel(
    n, own, nodes,
    length_ref, parents_ref, path_ref, q_ref, k_ref, v_ref, kc_ref, vc_ref, w_ref,
    att_ref, out_ref,
    qbuf, kbuf, vbuf, wbuf, bias, sbuf, lbuf, rbuf, rlbuf, acc,
    load_sem, q_load_sem, q_send, q_recv, p_send, p_recv, l_send, l_recv,
):
    me = lax.axis_index("blk")
    rows = q_ref.shape[0]
    wide = n * rows
    cached = kc_ref.shape[0]
    picked = path_ref.shape[0]
    peers = [lax.rem(me + k, n) for k in range(1, n)]

    q_loads = [
        pltpu.make_async_copy(
            q_ref.at[:, pl.ds(c * CHUNK, CHUNK)], qbuf.at[c, me], q_load_sem.at[c]
        )
        for c in range(CHUNKS)
    ]
    for copy in q_loads:
        copy.start()
    load_k = pltpu.make_async_copy(kc_ref, kbuf.at[pl.ds(0, cached)], load_sem.at[0])
    load_v = pltpu.make_async_copy(vc_ref, vbuf.at[pl.ds(0, cached)], load_sem.at[1])
    load_w = pltpu.make_async_copy(w_ref, wbuf, load_sem.at[2])
    load_k.start()
    load_v.start()
    load_w.start()

    barrier = pltpu.get_barrier_semaphore()
    for peer in peers:
        pl.semaphore_signal(barrier, inc=1, device_id={"blk": peer}, device_id_type=MESH)
    pl.semaphore_wait(barrier, n - 1)

    def q_copy(c, slot, peer):
        return pltpu.make_async_remote_copy(
            src_ref=qbuf.at[c, slot], dst_ref=qbuf.at[c, slot],
            send_sem=q_send.at[c, peer], recv_sem=q_recv.at[c, slot],
            device_id={"blk": peer}, device_id_type=MESH,
        )

    def p_copy(c, slot, peer):
        return pltpu.make_async_remote_copy(
            src_ref=sbuf.at[c, peer], dst_ref=rbuf.at[c, slot],
            send_sem=p_send.at[c, peer], recv_sem=p_recv.at[c, slot],
            device_id={"blk": peer}, device_id_type=MESH,
        )

    def l_copy(c, slot, peer):
        return pltpu.make_async_remote_copy(
            src_ref=lbuf.at[c, peer], dst_ref=rlbuf.at[c, slot],
            send_sem=l_send.at[c, peer], recv_sem=l_recv.at[c, slot],
            device_id={"blk": peer}, device_id_type=MESH,
        )

    for c in range(CHUNKS):
        q_loads[c].wait()
        for peer in peers:
            q_copy(c, me, peer).start()

    blank = jnp.zeros((LANES - rows, k_ref.shape[1]), jnp.float32)
    for ref, buf in ((k_ref, kbuf), (v_ref, vbuf)):
        buf[pl.ds(cached, LANES)] = jnp.concatenate(
            [ref[...].astype(jnp.float32), blank], axis=0
        ).astype(jnp.bfloat16)

    up = lax.broadcasted_iota(jnp.int32, (wide, wide), 0)
    down = lax.broadcasted_iota(jnp.int32, (wide, wide), 1)
    up_node = up // rows * own + up % rows
    links = jnp.where(up == down, 1.0, 0.0)
    for i in range(1, nodes):
        at = i // own * rows + i % own
        links = jnp.where((down == at) & (up_node == parents_ref[i]) & (up % rows < own), 1.0, links)
    for squaring in range(max(1, math.ceil(math.log2(nodes)))):
        half = links.astype(jnp.bfloat16)
        links = jnp.minimum(jnp.dot(half, half, preferred_element_type=jnp.float32), 1.0)
    source = lax.broadcasted_iota(jnp.int32, (wide, LANES), 0)
    column = lax.broadcasted_iota(jnp.int32, (wide, LANES), 1)
    mine = jnp.where((source == me * rows + column) & (column < own), 1.0, 0.0)
    related = lax.dot_general(
        links.astype(jnp.bfloat16), mine.astype(jnp.bfloat16), (((0,), (0,)), ((), ())),
        preferred_element_type=jnp.float32,
    )
    position = lax.broadcasted_iota(jnp.int32, (wide, cached), 1) + me * cached
    bias[:, pl.ds(0, cached)] = jnp.where(position < length_ref[0], 0.0, EXCLUDED)
    bias[:, pl.ds(cached, LANES)] = jnp.where(related > 0.5, 0.0, EXCLUDED)

    which = lax.broadcasted_iota(jnp.int32, (picked, wide), 0)
    spot = lax.broadcasted_iota(jnp.int32, (picked, wide), 1)
    spot_node = spot // rows * own + spot % rows
    wanted = jnp.full((picked, wide), -1, jnp.int32)
    for k in range(picked):
        wanted = jnp.where(which == k, path_ref[k], wanted)
    picker = jnp.where((wanted == spot_node) & (spot % rows < own), 1.0, 0.0)
    picker_half = picker.astype(jnp.bfloat16)

    load_k.wait()
    load_v.wait()
    lane = lax.broadcasted_iota(jnp.int32, (wide, LANES), 1)
    low = lane < HEAD_WIDTH

    def attend(c, unused):
        for peer in peers:
            q_copy(c, peer, peer).wait_recv()
        q = qbuf[c].astype(jnp.float32).reshape(wide, CHUNK)
        columns = pl.ds(pl.multiple_of(c * LANES, LANES), LANES)
        keys = kbuf[:, columns]
        values = vbuf[:, columns]
        tiles = []
        logs = jnp.full((wide, LANES), EXCLUDED, jnp.float32)
        for side in range(2):
            keep = low if side == 0 else jnp.logical_not(low)
            stacked = []
            for pair in range(PAIRS // 2):
                start = (side * PAIRS // 2 + pair) * LANES
                tile = q[:, start : start + LANES]
                turned = pltpu.roll(tile, HEAD_WIDTH, 1)
                even, odd = (tile, turned) if side == 0 else (turned, tile)
                stacked.append(jnp.where(keep, even, 0.0))
                stacked.append(jnp.where(keep, odd, 0.0))
            queries = jnp.concatenate(stacked, axis=0).astype(jnp.bfloat16)
            scores = lax.dot_general(queries, keys, NT, preferred_element_type=jnp.float32)
            scores = (
                scores.reshape(GROUP, wide, cached + LANES) + bias[...][None]
            ).reshape(GROUP * wide, cached + LANES)
            top = jnp.maximum(jnp.max(scores, axis=-1, keepdims=True), FLOOR)
            weights = jnp.exp2((scores - top) * (SCALE * math.log2(math.e)))
            total = jnp.sum(weights, axis=-1, keepdims=True)
            weighted = jnp.dot(
                weights.astype(jnp.bfloat16), values, preferred_element_type=jnp.float32
            )
            some = total > 0.0
            safe = jnp.where(some, total, 1.0)
            weighted = weighted / safe
            level = jnp.where(some, top * SCALE + jnp.log(safe), EXCLUDED)
            for head in range(GROUP):
                logs = jnp.where(
                    lane == side * GROUP + head, level[head * wide : (head + 1) * wide], logs
                )
            for pair in range(PAIRS // 2):
                even = weighted[2 * pair * wide : (2 * pair + 1) * wide]
                odd = weighted[(2 * pair + 1) * wide : (2 * pair + 2) * wide]
                if side == 0:
                    odd = pltpu.roll(odd, HEAD_WIDTH, 1)
                else:
                    even = pltpu.roll(even, HEAD_WIDTH, 1)
                tiles.append(jnp.where(low, even, odd))
        part = jnp.concatenate(tiles, axis=1)
        path_part = jnp.dot(
            picker_half, part.astype(jnp.bfloat16), preferred_element_type=jnp.float32
        )
        path_logs = jnp.dot(
            picker, logs, preferred_element_type=jnp.float32, precision=lax.Precision.HIGHEST
        )
        for d in range(n):
            mine = slice(d * rows, (d + 1) * rows)
            sbuf[c, d] = jnp.concatenate([part[mine], path_part], axis=0).astype(jnp.bfloat16)
            lbuf[c, d] = jnp.concatenate([logs[mine], path_logs], axis=0)
        for peer in peers:
            p_copy(c, me, peer).start()
            l_copy(c, me, peer).start()
        return unused

    lax.fori_loop(0, CHUNKS, attend, 0)
    load_w.wait()
    acc[...] = jnp.zeros_like(acc)
    low_out = lax.broadcasted_iota(jnp.int32, (rows + picked, LANES), 1) < HEAD_WIDTH

    def finish(c, unused):
        for peer in peers:
            p_copy(c, peer, peer).wait_recv()
            l_copy(c, peer, peer).wait_recv()
        logs = [lbuf[c, me]] + [rlbuf[c, peer] for peer in peers]
        parts = [sbuf[c, me]] + [rbuf[c, peer] for peer in peers]
        top = functools.reduce(jnp.maximum, logs)
        shares = [jnp.exp(log - top) for log in logs]
        total = functools.reduce(jnp.add, shares)
        shares = [share / total for share in shares]
        tiles = []
        for pair in range(PAIRS):
            span = slice(pair * LANES, (pair + 1) * LANES)
            tile = jnp.zeros((rows + picked, LANES), jnp.float32)
            for share, part in zip(shares, parts):
                factor = jnp.where(
                    low_out, share[:, 2 * pair : 2 * pair + 1], share[:, 2 * pair + 1 : 2 * pair + 2]
                )
                tile = tile + factor * part[:, span].astype(jnp.float32)
            tiles.append(tile)
        rows_done = jnp.concatenate(tiles, axis=1)
        columns = pl.ds(pl.multiple_of(c * CHUNK, CHUNK), CHUNK)
        att_ref[:, columns] = rows_done[:rows].astype(jnp.bfloat16)
        acc[...] += lax.dot_general(
            rows_done[rows:].astype(jnp.bfloat16), wbuf[:, columns], NT,
            preferred_element_type=jnp.float32,
        )
        return unused

    lax.fori_loop(0, CHUNKS, finish, 0)
    out_ref[...] = acc[...].astype(jnp.bfloat16)

    def drain(c, unused):
        for peer in peers:
            q_copy(c, me, peer).wait_send()
            p_copy(c, me, peer).wait_send()
            l_copy(c, me, peer).wait_send()
        return unused

    lax.fori_loop(0, CHUNKS, drain, 0)


def local(
    n,
    draft_node_queries,
    draft_node_keys,
    draft_node_values,
    paged_key_cache,
    paged_value_cache,
    context_length,
    parents,
    accepted_path,
    out_weight,
):
    own = draft_node_queries.shape[0]
    rows = -(-own // 8) * 8
    if rows != own:
        pad = ((0, rows - own), (0, 0))
        draft_node_queries = jnp.pad(draft_node_queries, pad)
        draft_node_keys = jnp.pad(draft_node_keys, pad)
        draft_node_values = jnp.pad(draft_node_values, pad)
    wide = n * rows
    cached, cache_width = paged_key_cache.shape
    picked = accepted_path.shape[0]
    smem = pl.BlockSpec(memory_space=pltpu.SMEM)
    vmem = pl.BlockSpec(memory_space=pltpu.VMEM)
    anywhere = pl.BlockSpec(memory_space=pl.ANY)
    attention, path_output = pl.pallas_call(
        functools.partial(kernel, n, own, parents.shape[0]),
        out_shape=(
            jax.ShapeDtypeStruct((rows, QUERY_HEADS * HEAD_WIDTH), jnp.bfloat16),
            jax.ShapeDtypeStruct((picked, out_weight.shape[0]), jnp.bfloat16),
        ),
        in_specs=[smem] * 3 + [anywhere, vmem, vmem] + [anywhere] * 3,
        out_specs=(vmem, vmem),
        scratch_shapes=[
            pltpu.VMEM((CHUNKS, n, rows, CHUNK), jnp.bfloat16),
            pltpu.VMEM((cached + LANES, cache_width), jnp.bfloat16),
            pltpu.VMEM((cached + LANES, cache_width), jnp.bfloat16),
            pltpu.VMEM(out_weight.shape, jnp.bfloat16),
            pltpu.VMEM((wide, cached + LANES), jnp.float32),
            pltpu.VMEM((CHUNKS, n, rows + picked, CHUNK), jnp.bfloat16),
            pltpu.VMEM((CHUNKS, n, rows + picked, LANES), jnp.float32),
            pltpu.VMEM((CHUNKS, n, rows + picked, CHUNK), jnp.bfloat16),
            pltpu.VMEM((CHUNKS, n, rows + picked, LANES), jnp.float32),
            pltpu.VMEM((picked, out_weight.shape[0]), jnp.float32),
            pltpu.SemaphoreType.DMA((3,)),
            pltpu.SemaphoreType.DMA((CHUNKS,)),
        ]
        + [pltpu.SemaphoreType.DMA((CHUNKS, n))] * 6,
        compiler_params=pltpu.CompilerParams(
            collective_id=0, has_side_effects=True, vmem_limit_bytes=56 * 1024 * 1024
        ),
        name="verify_tree",
    )(
        context_length, parents, accepted_path,
        draft_node_queries, draft_node_keys, draft_node_values,
        paged_key_cache, paged_value_cache, out_weight,
    )
    return attention[:own], path_output


def solution(mesh):
    in_specs = (
        P(("req", "blk"), None),
        P(("req", "blk"), None),
        P(("req", "blk"), None),
        P(("req", "blk"), None),
        P(("req", "blk"), None),
        P("req"),
        P("req"),
        P("req"),
        P("blk", None),
    )
    out_specs = (P(("req", "blk"), None), P("req", "blk"))
    return jax.shard_map(
        functools.partial(local, mesh.shape["blk"]),
        mesh=mesh, in_specs=in_specs, out_specs=out_specs, check_vma=False,
    )
```

time: 79.5 us -> 23.9 us (0.30)
  blocking collectives: 37 us -> 0 us
  Pallas kernels: 0 us -> 19.6 us
  matrix products: 10.1 us -> 0 us
  starting transfers between devices: 9.98 us -> 0 us
  local copies, waits for them, and re-layouts: 9.31 us -> 2.78 us
  other arithmetic: 5.63 us -> 0 us
  waiting for transfers between devices: 5.21 us -> 0 us
    all_gather x4 -> x0, blocking collectives: 37 us -> none  [the longest x1 10.8 us: local(): lax.all_gather(draft_node_queries, 'blk', axis=0, tiled=True)]
    pallas_call x0 -> x1, Pallas kernels: none -> 19.6 us  [local(): pl.pallas_call(functools.partial(kernel, n, own, parents.shape[0]), out_s...]
    dot_general x12 -> x0, matrix products: 10.1 us -> none  [the longest x1 5.04 us: local(): lax.dot_general(path_rows, out_weight, (((1,), (1,)), ((), ())), preferre...]
    all_to_all x3 -> x0, starting transfers between devices: 9.98 us -> none  [the longest x1 3.48 us: local(): lax.all_to_all(partial_value[2][None], 'blk', split_axis=1, concat_axis=0...]
    all_to_all x3 -> x0, waiting for transfers between devices: 5.21 us -> none  [the longest x1 5.21 us: local(): lax.all_to_all(partial_value[2][None], 'blk', split_axis=1, concat_axis=0...]
    all_to_all x3 -> x0, other arithmetic: 3.49 us -> none  [the longest x1 2.14 us: local(): lax.all_to_all(partial_value[2][None], 'blk', split_axis=1, concat_axis=0...]
    unnamed x24 -> x2, local copies, waits for them, and re-layouts: 6.08 us -> 2.78 us
    reduce_sum x4 -> x0, other arithmetic: 2.03 us -> none  [the longest x2 1.65 us: fold_block(): totals = totals * rescale + jnp.sum(weights, axis=-1)]
  transfers between devices with their start and end apart: 3 -> 0, of which waited for: 1 -> 0; matrix products, arithmetic and copies ran while one was open for 14% -> 0% of each run, Pallas kernels for 0% -> 0%
where the time goes in v1:
time: 23.9 us; the launch traced here: 23.6 us
  Pallas kernels  19.6 us (82%)
  local copies, waits for them, and re-layouts  2.78 us (12%)
  between operations  1.29 us (5%)
    pallas_call x1, Pallas kernels, local(): pl.pallas_call(functools.partial(kernel, n, own, parents.shape[0]), out_s...  19.6 us
    unnamed x2, local copies, waits for them, and re-layouts  2.78 us

profile of v1, /device:TPU:0, one launch (start us, length us, event | category | flops | bytes accessed | tf_op | source)
XLA Modules:
  0.0 23.6 jit_solution(2201095796095218186)
XLA Ops:
  1.3 19.6 %verify_tree.1 = (bf16[8,4096]{1,0:T(8,128)(2,1)}, bf16[8,720]{1,0:T(8,128)(2,1)}) custom-call(s32[1]{0:T(128)S(6)} %copy.13.length_ref, s32[32]{0:T(128)} %parents_ref.1, s32[8]{0:T(128)} %path_ref.1, bf16[8,4096]{1,0:T(8,128)(2,1)} %q_ref.1, bf16[8,512]{1,0:T(8,128)(2,1)} %k_ref.1, bf16[8,512]{1,0:T(8,128)(2,1)} %v_ref.1, bf16[512,512]{1,0:T(8,128)(2,1)} %kc_ref.1, ...), custom_call_target="tpu_custom_call" | custom-call | tf_op jit(solution)/shard_map/verify_tree/pallas_call | solution.py:261
  20.9 1.5 %copy.14 = bf16[8,4096]{1,0:T(8,128)(2,1)} copy(bf16[8,4096]{1,0:T(8,128)(2,1)} %get-tuple-element.4) | data formatting | bytes 131072
  22.3 1.3 %copy.15 = bf16[8,720]{1,0:T(8,128)(2,1)} copy(bf16[8,720]{1,0:T(8,128)(2,1)} %get-tuple-element.5) | data formatting | bytes 23040

commit v2 on v1

--- a/solution.py
+++ b/solution.py
@@ -16,6 +16,7 @@
 CHUNKS = KEY_VALUE_HEADS * HEAD_WIDTH // LANES
 CHUNK = 2 * GROUP * HEAD_WIDTH
 PAIRS = CHUNK // LANES
+HEADS = 2 * GROUP
 EXCLUDED = -1e30
 FLOOR = -1e20
 SCALE = HEAD_WIDTH ** (-0.5)
@@ -25,16 +26,17 @@
 
 def kernel(
     n, own, nodes,
-    length_ref, parents_ref, path_ref, q_ref, k_ref, v_ref, kc_ref, vc_ref, w_ref,
+    length_hbm, parents_hbm, path_hbm, q_ref, k_ref, v_ref, kc_ref, vc_ref, w_ref,
     att_ref, out_ref,
-    qbuf, kbuf, vbuf, wbuf, bias, sbuf, lbuf, rbuf, rlbuf, acc,
-    load_sem, q_load_sem, q_send, q_recv, p_send, p_recv, l_send, l_recv,
+    length_ref, parents_ref, path_ref, kown, vown,
+    qbuf, kbuf, vbuf, wbuf, bias, sbuf, rbuf, acc,
+    load_sem, q_load_sem, q_send, q_recv, p_send, p_recv,
 ):
     me = lax.axis_index("blk")
     rows = q_ref.shape[0]
     wide = n * rows
     cached = kc_ref.shape[0]
-    picked = path_ref.shape[0]
+    picked = path_hbm.shape[0]
     peers = [lax.rem(me + k, n) for k in range(1, n)]
 
     q_loads = [
@@ -44,6 +46,15 @@
         for c in range(CHUNKS)
     ]
     for copy in q_loads:
+        copy.start()
+    small_loads = [
+        pltpu.make_async_copy(src, dst, load_sem.at[3 + i])
+        for i, (src, dst) in enumerate((
+            (parents_hbm, parents_ref), (length_hbm, length_ref), (path_hbm, path_ref),
+            (k_ref, kown), (v_ref, vown),
+        ))
+    ]
+    for copy in small_loads:
         copy.start()
     load_k = pltpu.make_async_copy(kc_ref, kbuf.at[pl.ds(0, cached)], load_sem.at[0])
     load_v = pltpu.make_async_copy(vc_ref, vbuf.at[pl.ds(0, cached)], load_sem.at[1])
@@ -71,20 +82,15 @@
             device_id={"blk": peer}, device_id_type=MESH,
         )
 
-    def l_copy(c, slot, peer):
-        return pltpu.make_async_remote_copy(
-            src_ref=lbuf.at[c, peer], dst_ref=rlbuf.at[c, slot],
-            send_sem=l_send.at[c, peer], recv_sem=l_recv.at[c, slot],
-            device_id={"blk": peer}, device_id_type=MESH,
-        )
-
     for c in range(CHUNKS):
         q_loads[c].wait()
         for peer in peers:
             q_copy(c, me, peer).start()
 
+    for copy in small_loads:
+        copy.wait()
     blank = jnp.zeros((LANES - rows, k_ref.shape[1]), jnp.float32)
-    for ref, buf in ((k_ref, kbuf), (v_ref, vbuf)):
+    for ref, buf in ((kown, kbuf), (vown, vbuf)):
         buf[pl.ds(cached, LANES)] = jnp.concatenate(
             [ref[...].astype(jnp.float32), blank], axis=0
         ).astype(jnp.bfloat16)
@@ -170,20 +176,28 @@
                 else:
                     even = pltpu.roll(even, HEAD_WIDTH, 1)
                 tiles.append(jnp.where(low, even, odd))
+        first = logs.astype(jnp.bfloat16).astype(jnp.float32)
+        rest = logs - first
+        second = rest.astype(jnp.bfloat16).astype(jnp.float32)
+        third = rest - second
+        tiles.append(
+            jnp.where(
+                lane < HEADS, first,
+                jnp.where(
+                    lane < 2 * HEADS, pltpu.roll(second, HEADS, 1),
+                    jnp.where(lane < 3 * HEADS, pltpu.roll(third, 2 * HEADS, 1), 0.0),
+                ),
+            )
+        )
         part = jnp.concatenate(tiles, axis=1)
         path_part = jnp.dot(
             picker_half, part.astype(jnp.bfloat16), preferred_element_type=jnp.float32
         )
-        path_logs = jnp.dot(
-            picker, logs, preferred_element_type=jnp.float32, precision=lax.Precision.HIGHEST
-        )
         for d in range(n):
             mine = slice(d * rows, (d + 1) * rows)
             sbuf[c, d] = jnp.concatenate([part[mine], path_part], axis=0).astype(jnp.bfloat16)
-            lbuf[c, d] = jnp.concatenate([logs[mine], path_logs], axis=0)
         for peer in peers:
             p_copy(c, me, peer).start()
-            l_copy(c, me, peer).start()
         return unused
 
     lax.fori_loop(0, CHUNKS, attend, 0)
@@ -194,9 +208,15 @@
     def finish(c, unused):
         for peer in peers:
             p_copy(c, peer, peer).wait_recv()
-            l_copy(c, peer, peer).wait_recv()
-        logs = [lbuf[c, me]] + [rlbuf[c, peer] for peer in peers]
         parts = [sbuf[c, me]] + [rbuf[c, peer] for peer in peers]
+        logs = []
+        for part in parts:
+            terms = part[:, CHUNK:].astype(jnp.float32)
+            logs.append(
+                terms
+                + pltpu.roll(terms, LANES - HEADS, 1)
+                + pltpu.roll(terms, LANES - 2 * HEADS, 1)
+            )
         top = functools.reduce(jnp.maximum, logs)
         shares = [jnp.exp(log - top) for log in logs]
         total = functools.reduce(jnp.add, shares)
@@ -227,10 +247,20 @@
         for peer in peers:
             q_copy(c, me, peer).wait_send()
             p_copy(c, me, peer).wait_send()
-            l_copy(c, me, peer).wait_send()
         return unused
 
     lax.fori_loop(0, CHUNKS, drain, 0)
+
+
+def write_out(att_ref, out_ref, att_hbm, out_hbm, sems):
+    copies = [
+        pltpu.make_async_copy(att_ref, att_hbm, sems.at[0]),
+        pltpu.make_async_copy(out_ref, out_hbm, sems.at[1]),
+    ]
+    for copy in copies:
+        copy.start()
+    for copy in copies:
+        copy.wait()
 
 
 def local(
@@ -255,32 +285,35 @@
     wide = n * rows
     cached, cache_width = paged_key_cache.shape
     picked = accepted_path.shape[0]
-    smem = pl.BlockSpec(memory_space=pltpu.SMEM)
     vmem = pl.BlockSpec(memory_space=pltpu.VMEM)
-    anywhere = pl.BlockSpec(memory_space=pl.ANY)
-    attention, path_output = pl.pallas_call(
+    anywhere = pl.BlockSpec(memory_space=pltpu.HBM)
+    shapes = (
+        jax.ShapeDtypeStruct((rows, QUERY_HEADS * HEAD_WIDTH), jnp.bfloat16),
+        jax.ShapeDtypeStruct((picked, out_weight.shape[0]), jnp.bfloat16),
+    )
+    held = pl.pallas_call(
         functools.partial(kernel, n, own, parents.shape[0]),
-        out_shape=(
-            jax.ShapeDtypeStruct((rows, QUERY_HEADS * HEAD_WIDTH), jnp.bfloat16),
-            jax.ShapeDtypeStruct((picked, out_weight.shape[0]), jnp.bfloat16),
-        ),
-        in_specs=[smem] * 3 + [anywhere, vmem, vmem] + [anywhere] * 3,
+        out_shape=tuple(pltpu.VMEM(shape.shape, shape.dtype) for shape in shapes),
+        in_specs=[anywhere] * 9,
         out_specs=(vmem, vmem),
         scratch_shapes=[
+            pltpu.SMEM(context_length.shape, jnp.int32),
+            pltpu.SMEM(parents.shape, jnp.int32),
+            pltpu.SMEM(accepted_path.shape, jnp.int32),
+            pltpu.VMEM((rows, cache_width), jnp.bfloat16),
+            pltpu.VMEM((rows, cache_width), jnp.bfloat16),
             pltpu.VMEM((CHUNKS, n, rows, CHUNK), jnp.bfloat16),
             pltpu.VMEM((cached + LANES, cache_width), jnp.bfloat16),
             pltpu.VMEM((cached + LANES, cache_width), jnp.bfloat16),
             pltpu.VMEM(out_weight.shape, jnp.bfloat16),
             pltpu.VMEM((wide, cached + LANES), jnp.float32),
-            pltpu.VMEM((CHUNKS, n, rows + picked, CHUNK), jnp.bfloat16),
-            pltpu.VMEM((CHUNKS, n, rows + picked, LANES), jnp.float32),
-            pltpu.VMEM((CHUNKS, n, rows + picked, CHUNK), jnp.bfloat16),
-            pltpu.VMEM((CHUNKS, n, rows + picked, LANES), jnp.float32),
+            pltpu.VMEM((CHUNKS, n, rows + picked, CHUNK + LANES), jnp.bfloat16),
+            pltpu.VMEM((CHUNKS, n, rows + picked, CHUNK + LANES), jnp.bfloat16),
             pltpu.VMEM((picked, out_weight.shape[0]), jnp.float32),
-            pltpu.SemaphoreType.DMA((3,)),
+            pltpu.SemaphoreType.DMA((8,)),
             pltpu.SemaphoreType.DMA((CHUNKS,)),
         ]
-        + [pltpu.SemaphoreType.DMA((CHUNKS, n))] * 6,
+        + [pltpu.SemaphoreType.DMA((CHUNKS, n))] * 4,
         compiler_params=pltpu.CompilerParams(
             collective_id=0, has_side_effects=True, vmem_limit_bytes=56 * 1024 * 1024
         ),
@@ -290,6 +323,15 @@
         draft_node_queries, draft_node_keys, draft_node_values,
         paged_key_cache, paged_value_cache, out_weight,
     )
+    attention, path_output = pl.pallas_call(
+        write_out,
+        out_shape=shapes,
+        in_specs=(vmem, vmem),
+        out_specs=(anywhere, anywhere),
+        scratch_shapes=[pltpu.SemaphoreType.DMA((2,))],
+        compiler_params=pltpu.CompilerParams(vmem_limit_bytes=1024 * 1024),
+        name="write_out",
+    )(*held)
     return attention[:own], path_output
 
 

time: 23.9 us -> 19.7 us (0.82)
  local copies, waits for them, and re-layouts: 2.78 us -> 0 us
  Pallas kernels: 19.6 us -> 18.2 us
    unnamed x2 -> x0, local copies, waits for them, and re-layouts: 2.78 us -> none
    pallas_call x1, Pallas kernels: 19.6 us -> 17.6 us  [local(): pl.pallas_call(functools.partial(kernel, n, own, parents.shape[0]), out_s...]
    pallas_call x0 -> x1, Pallas kernels: none -> 0.65 us  [local(): pl.pallas_call(write_out, out_shape=shapes, in_specs=(vmem, vmem), out_sp...]
where the time goes in v2:
time: 19.7 us; the launch traced here: 19.5 us
  Pallas kernels  18.2 us (92%)
  between operations  1.29 us (7%)
    pallas_call x1, Pallas kernels, local(): pl.pallas_call(functools.partial(kernel, n, own, parents.shape[0]), out_s...  17.6 us
    pallas_call x1, Pallas kernels, local(): pl.pallas_call(write_out, out_shape=shapes, in_specs=(vmem, vmem), out_sp...  0.65 us

profile of v2, /device:TPU:0, one launch (start us, length us, event | category | flops | bytes accessed | tf_op | source)
XLA Modules:
  0.0 19.5 jit_solution(4573255615958572893)
XLA Ops:
  1.3 17.6 %verify_tree.1 = (bf16[8,4096]{1,0:T(8,128)(2,1)S(1)}, bf16[8,720]{1,0:T(8,128)(2,1)S(1)}) custom-call(s32[1]{0:T(128)S(6)} %copy.11.length_hbm, s32[32]{0:T(128)} %parents_hbm.1, s32[8]{0:T(128)} %path_hbm.1, bf16[8,4096]{1,0:T(8,128)(2,1)} %q_ref.1, bf16[8,512]{1,0:T(8,128)(2,1)} %k_ref.1, bf16[8,512]{1,0:T(8,128)(2,1)} %v_ref.1, bf16[512,512]{1,0:T(8,128)(2,1)} %kc_ref.1, ...), custom_call_target="tpu_custom_call" | custom-call | tf_op jit(solution)/shard_map/verify_tree/pallas_call | solution.py:294
  18.8 0.7 %write_out.1 = (bf16[8,4096]{1,0:T(8,128)(2,1)}, bf16[8,720]{1,0:T(8,128)(2,1)}) custom-call(bf16[8,4096]{1,0:T(8,128)(2,1)S(1)} %get-tuple-element.4.att_ref, bf16[8,720]{1,0:T(8,128)(2,1)S(1)} %get-tuple-element.5.out_ref), custom_call_target="tpu_custom_call" | custom-call | tf_op jit(solution)/shard_map/write_out/pallas_call | solution.py:326

commit v3 on v2

--- a/solution.py
+++ b/solution.py
@@ -24,6 +24,18 @@
 MESH = pl.DeviceIdType.MESH
 
 
+def partner(me, k, n):
+    if n & (n - 1):
+        return lax.rem(me + k, n)
+    other = me
+    bit = 1
+    while bit < n:
+        if k & bit:
+            other = other + bit - 2 * bit * ((me // bit) % 2)
+        bit *= 2
+    return other
+
+
 def kernel(
     n, own, nodes,
     length_hbm, parents_hbm, path_hbm, q_ref, k_ref, v_ref, kc_ref, vc_ref, w_ref,
@@ -37,7 +49,7 @@
     wide = n * rows
     cached = kc_ref.shape[0]
     picked = path_hbm.shape[0]
-    peers = [lax.rem(me + k, n) for k in range(1, n)]
+    peers = [partner(me, k, n) for k in range(n - 1, 0, -1)]
 
     q_loads = [
         pltpu.make_async_copy(
@@ -47,6 +59,10 @@
     ]
     for copy in q_loads:
         copy.start()
+    load_k = pltpu.make_async_copy(kc_ref, kbuf.at[pl.ds(0, cached)], load_sem.at[0])
+    load_v = pltpu.make_async_copy(vc_ref, vbuf.at[pl.ds(0, cached)], load_sem.at[1])
+    load_w = pltpu.make_async_copy(w_ref, wbuf, load_sem.at[2])
+
     small_loads = [
         pltpu.make_async_copy(src, dst, load_sem.at[3 + i])
         for i, (src, dst) in enumerate((
@@ -56,12 +72,6 @@
     ]
     for copy in small_loads:
         copy.start()
-    load_k = pltpu.make_async_copy(kc_ref, kbuf.at[pl.ds(0, cached)], load_sem.at[0])
-    load_v = pltpu.make_async_copy(vc_ref, vbuf.at[pl.ds(0, cached)], load_sem.at[1])
-    load_w = pltpu.make_async_copy(w_ref, wbuf, load_sem.at[2])
-    load_k.start()
-    load_v.start()
-    load_w.start()
 
     barrier = pltpu.get_barrier_semaphore()
     for peer in peers:
@@ -86,6 +96,9 @@
         q_loads[c].wait()
         for peer in peers:
             q_copy(c, me, peer).start()
+    load_k.start()
+    load_v.start()
+    load_w.start()
 
     for copy in small_loads:
         copy.wait()

time: 19.7 us -> 19.4 us (0.985)
  Pallas kernels: 18.2 us -> 17.9 us
    pallas_call x1, Pallas kernels: 17.6 us -> 17.3 us  [local(): pl.pallas_call(functools.partial(kernel, n, own, parents.shape[0]), out_s...]
where the time goes in v3:
time: 19.4 us; the launch traced here: 19.2 us
  Pallas kernels  17.9 us (92%)
  between operations  1.29 us (7%)
    pallas_call x1, Pallas kernels, local(): pl.pallas_call(functools.partial(kernel, n, own, parents.shape[0]), out_s...  17.3 us
    pallas_call x1, Pallas kernels, local(): pl.pallas_call(write_out, out_shape=shapes, in_specs=(vmem, vmem), out_sp...  0.65 us

profile of v3, /device:TPU:0, one launch (start us, length us, event | category | flops | bytes accessed | tf_op | source)
XLA Modules:
  0.0 19.2 jit_solution(1944170124560121956)
XLA Ops:
  1.3 17.3 %verify_tree.1 = (bf16[8,4096]{1,0:T(8,128)(2,1)S(1)}, bf16[8,720]{1,0:T(8,128)(2,1)S(1)}) custom-call(s32[1]{0:T(128)S(6)} %copy.11.length_hbm, s32[32]{0:T(128)} %parents_hbm.1, s32[8]{0:T(128)} %path_hbm.1, bf16[8,4096]{1,0:T(8,128)(2,1)} %q_ref.1, bf16[8,512]{1,0:T(8,128)(2,1)} %k_ref.1, bf16[8,512]{1,0:T(8,128)(2,1)} %v_ref.1, bf16[512,512]{1,0:T(8,128)(2,1)} %kc_ref.1, ...), custom_call_target="tpu_custom_call" | custom-call | tf_op jit(solution)/shard_map/verify_tree/pallas_call | solution.py:307
  18.6 0.7 %write_out.1 = (bf16[8,4096]{1,0:T(8,128)(2,1)}, bf16[8,720]{1,0:T(8,128)(2,1)}) custom-call(bf16[8,4096]{1,0:T(8,128)(2,1)S(1)} %get-tuple-element.4.att_ref, bf16[8,720]{1,0:T(8,128)(2,1)S(1)} %get-tuple-element.5.out_ref), custom_call_target="tpu_custom_call" | custom-call | tf_op jit(solution)/shard_map/write_out/pallas_call | solution.py:339

commit v4 on v3

--- a/solution.py
+++ b/solution.py
@@ -213,7 +213,7 @@
             p_copy(c, me, peer).start()
         return unused
 
-    lax.fori_loop(0, CHUNKS, attend, 0)
+    lax.fori_loop(0, CHUNKS, attend, 0, unroll=True)
     load_w.wait()
     acc[...] = jnp.zeros_like(acc)
     low_out = lax.broadcasted_iota(jnp.int32, (rows + picked, LANES), 1) < HEAD_WIDTH
@@ -253,7 +253,7 @@
         )
         return unused
 
-    lax.fori_loop(0, CHUNKS, finish, 0)
+    lax.fori_loop(0, CHUNKS, finish, 0, unroll=True)
     out_ref[...] = acc[...].astype(jnp.bfloat16)
 
     def drain(c, unused):

time: 19.4 us -> 19.4 us (level)
  no operation moved by 1% of the time
where the time goes in v4:
time: 19.4 us; the launch traced here: 19.2 us
  Pallas kernels  17.9 us (92%)
  between operations  1.29 us (7%)
    pallas_call x1, Pallas kernels, local(): pl.pallas_call(functools.partial(kernel, n, own, parents.shape[0]), out_s...  17.3 us
    pallas_call x1, Pallas kernels, local(): pl.pallas_call(write_out, out_shape=shapes, in_specs=(vmem, vmem), out_sp...  0.65 us

profile of v4, /device:TPU:0, one launch (start us, length us, event | category | flops | bytes accessed | tf_op | source)
XLA Modules:
  0.0 19.2 jit_solution(11434262040569546139)
XLA Ops:
  1.3 17.3 %verify_tree.1 = (bf16[8,4096]{1,0:T(8,128)(2,1)S(1)}, bf16[8,720]{1,0:T(8,128)(2,1)S(1)}) custom-call(s32[1]{0:T(128)S(6)} %copy.11.length_hbm, s32[32]{0:T(128)} %parents_hbm.1, s32[8]{0:T(128)} %path_hbm.1, bf16[8,4096]{1,0:T(8,128)(2,1)} %q_ref.1, bf16[8,512]{1,0:T(8,128)(2,1)} %k_ref.1, bf16[8,512]{1,0:T(8,128)(2,1)} %v_ref.1, bf16[512,512]{1,0:T(8,128)(2,1)} %kc_ref.1, ...), custom_call_target="tpu_custom_call" | custom-call | tf_op jit(solution)/shard_map/verify_tree/pallas_call | solution.py:307
  18.6 0.7 %write_out.1 = (bf16[8,4096]{1,0:T(8,128)(2,1)}, bf16[8,720]{1,0:T(8,128)(2,1)}) custom-call(bf16[8,4096]{1,0:T(8,128)(2,1)S(1)} %get-tuple-element.4.att_ref, bf16[8,720]{1,0:T(8,128)(2,1)S(1)} %get-tuple-element.5.out_ref), custom_call_target="tpu_custom_call" | custom-call | tf_op jit(solution)/shard_map/write_out/pallas_call | solution.py:339
